TPU v7x, 32 devices: a whole 2x2x4 slice. The times are simulated.
32 devices in a mesh: parts: 2 (over y), ep: 16 (over z, x, core).
Axes of the slice: x: 2, y: 2, z: 4, core: 2. Of those that a mesh axis runs over, the one named last changes fastest.
Arguments:
- tokens: bfloat16 [512, 2048], P(('parts', 'ep')), parts along dimension 0, may hold values from -6 to 6
- gate_up: bfloat16 [4096, 16, 1536], P(('parts', 'ep')), parts along dimension 0, may hold values from -0.125 to 0.125
- down_proj: bfloat16 [1536, 16, 2048], P(('parts', 'ep')), parts along dimension 0, may hold values from -0.21875 to 0.21875
- expert_ids: int32 [512, 8], P(('parts', 'ep')), parts along dimension 0, may hold values from 0 to 15, all different within a row; in each aligned block of 16 rows (0 to 15, 16 to 31, ...) at most 16 rows name the same one
- gate_weights: float32 [512, 8], P(('parts', 'ep')), parts along dimension 0, may hold values from 0.03 to 0.6
- owner_slot: int32 [32], P('parts'), parts along dimension 0, may hold values from 0 to 15, each once
Outputs:
- moe_out: bfloat16 [512, 2048], P(('parts', 'ep')), parts along dimension 0
- channel_scale: float32 [32, 3584], P(('parts', 'ep')), parts along dimension 0
There are 2 independent parts, one for each index of `parts`. A program takes and returns all parts, laid end to end along the dimension named above; each array names one. Nothing has to cross between parts.
Inputs may be any that keep to these rules, and one draw needn't show every extreme that they name: `expert_ids`: each row names 8 different experts; among the rows of one device no expert is named more than 16 times, a bound that some block reaches. `owner_slot`: A permutation: each slot holds exactly one expert.
All inputs are finite; a program needn't handle non-finite values.
Results may differ from a plain program's by a relative error of at most 0.0058.
Values may be sent and summed in bfloat16 or wider, within the bound.
A program may use at most 128 MiB of HBM per device.

v0:
```python
import functools
import math

import jax
import jax.numpy as jnp
from jax import lax
from jax.experimental import pallas as pl
from jax.experimental.pallas import tpu as pltpu
from jax.sharding import PartitionSpec as P


def expert_block(arrived, held_up, held_down):
    hidden = jnp.einsum("rjd,djf->rjf", arrived, held_up, preferred_element_type=jnp.float32)
    ffn_width = held_up.shape[2] // 2
    activated = (jax.nn.silu(hidden[..., :ffn_width]) * hidden[..., ffn_width:]).astype(
        jnp.bfloat16
    )
    return jnp.einsum(
        "rjf,fjd->rjd", activated, held_down, preferred_element_type=jnp.float32
    ).astype(jnp.bfloat16)


def column_scales(gate_up, down_proj):
    gate_scale = jnp.max(jnp.abs(gate_up), axis=0).astype(jnp.float32) * math.sqrt(gate_up.shape[0])
    down_scale = jnp.max(jnp.abs(down_proj), axis=0).astype(jnp.float32) * math.sqrt(
        down_proj.shape[0]
    )
    return jnp.concatenate([gate_scale, down_scale], axis=1)


def shards(tokens, gate_up, down_proj, expert_ids, gate_weights, owner_slot):
    tok_rows, model_width = tokens.shape
    top_count = expert_ids.shape[1]
    slots_all = gate_up.shape[1]
    devices = lax.axis_size("ep")
    own_count = slots_all // devices
    capacity = 2 * tok_rows * top_count // slots_all
    experts_iota = jnp.arange(slots_all, dtype=jnp.int32)
    inverse = jnp.zeros((slots_all,), jnp.int32).at[owner_slot].set(experts_iota)
    flat_ids = expert_ids.reshape(-1)
    one_hot = (flat_ids[:, None] == experts_iota[None, :]).astype(jnp.int32)
    slot_rank = jnp.sum((jnp.cumsum(one_hot, axis=0) - 1) * one_hot, axis=1)
    position = slot_rank * slots_all + flat_ids
    source_rows = jnp.repeat(tokens, top_count, axis=0)
    outbox = (
        jnp.zeros((capacity * slots_all, model_width), jnp.bfloat16).at[position].set(source_rows)
    )
    outbox = outbox.reshape(capacity, slots_all, model_width)
    held_up, held_down = (
        lax.all_to_all(gate_up, "ep", split_axis=1, concat_axis=0, tiled=True),
        lax.all_to_all(down_proj, "ep", split_axis=1, concat_axis=0, tiled=True),
    )
    arrived = lax.all_to_all(outbox, "ep", split_axis=1, concat_axis=0, tiled=True)
    expert_out = expert_block(arrived, held_up, held_down)
    returned = lax.all_to_all(expert_out, "ep", split_axis=0, concat_axis=1, tiled=True).reshape(
        capacity * slots_all, model_width
    )
    picked = returned[position].astype(jnp.float32).reshape(tok_rows, top_count, model_width)
    moe_out = jnp.sum(picked * gate_weights[:, :, None], axis=1).astype(jnp.bfloat16)
    scales = column_scales(held_up, held_down)
    every_row = lax.all_gather(scales, "ep", axis=0, tiled=True)
    mine = lax.dynamic_slice_in_dim(inverse, lax.axis_index("ep") * own_count, own_count)
    scales = jnp.take(every_row, mine, axis=0)
    return (moe_out, scales)


MESH = pl.DeviceIdType.MESH
F32, BF16 = jnp.float32, jnp.bfloat16


def fused_kernel(
    dims, tok_ref, ids_ref, gate_ref, slot_ref, up_hbm, down_hbm, out_ref, scale_ref,
    w_ref, wt_ref, d_ref, meta32, meta_ref, tok_all, tok_t, meta_all, id_row, gate_row, x_ref,
    h_ref, act_ref, a_ref, o_ref, out32, s_send, s_recv, *rest,
):
    n, bits, chunks, groups = dims
    hs, hr = rest[:bits], rest[bits : 2 * bits]
    os_, or_ = rest[2 * bits : 3 * bits], rest[3 * bits : 4 * bits]
    load_sem, small_send, small_recv, h_ssem, h_rsem, o_ssem, o_rsem = rest[4 * bits :]
    me = lax.axis_index("ep")
    own = tok_ref.shape[0]
    total = tok_all.shape[0]
    depth = tok_all.shape[1]
    experts = slot_ref.shape[1]
    top = ids_ref.shape[1]
    per = chunks // groups
    span = total // groups
    copies = total // span
    small = own // groups
    half = w_ref.shape[1] // 2
    fl = half // n
    width = d_ref.shape[1]
    root_d, root_f = math.sqrt(depth * n), math.sqrt(fl * n)

    load_w = pltpu.make_async_copy(up_hbm, w_ref, load_sem.at[0])
    load_d = pltpu.make_async_copy(down_hbm, d_ref, load_sem.at[1])
    load_w.start()
    load_d.start()

    meta32[...] = jnp.zeros_like(meta32)
    gates = gate_ref[...]
    meta32[:, 0:top] = ids_ref[...].astype(F32)
    for piece in range(1, 4):
        high = gates.astype(BF16).astype(F32)
        meta32[:, piece * top : (piece + 1) * top] = high
        gates = gates - high
    meta_ref[...] = meta32[...].astype(BF16)

    barrier = pltpu.get_barrier_semaphore()
    for i in range(1, n):
        pl.semaphore_signal(
            barrier, inc=1, device_id={"ep": lax.rem(me + i, n)}, device_id_type=MESH
        )
    pl.semaphore_wait(barrier, n - 1)

    def remote(src, dst, ssem, rsem, peer):
        return pltpu.make_async_remote_copy(
            src_ref=src, dst_ref=dst, send_sem=ssem, recv_sem=rsem,
            device_id={"ep": peer}, device_id_type=MESH,
        )

    mine = pl.ds(pl.multiple_of(me * own, own), own)

    def tok_copy(i):
        peer = lax.rem(me + i, n)
        cols = pl.ds(pl.multiple_of(peer * depth, depth), depth)
        return remote(
            tok_ref.at[:, cols], tok_all.at[mine, :], small_send.at[0, i], small_recv.at[0, i], peer
        )

    def meta_copy(i):
        peer = lax.rem(me + i, n)
        return remote(
            meta_ref, meta_all.at[mine, :], small_send.at[1, i], small_recv.at[1, i], peer
        )

    def scale_copy(i):
        peer = lax.rem(me + i, n)
        return remote(
            s_send.at[peer], s_recv.at[me], small_send.at[2, i], small_recv.at[2, i], peer
        )

    for i in range(1, n):
        meta_copy(i).start()
        tok_copy(i).start()
    tok_all[mine, :] = tok_ref[:, pl.ds(pl.multiple_of(me * depth, depth), depth)]
    meta_all[mine, :] = meta_ref[...]
    a_ref[...] = jnp.zeros_like(a_ref)

    def scales_in():
        def up_max(r, best):
            rows = pl.ds(pl.multiple_of(r * experts, experts), experts)
            return jnp.maximum(best, jnp.abs(w_ref[rows, :]))

        def down_max(r, best):
            rows = pl.ds(pl.multiple_of(r * experts, experts), experts)
            return jnp.maximum(best, jnp.abs(d_ref[rows, :]))

        choose = (
            lax.broadcasted_iota(jnp.int32, (experts, experts), 0)
            == jnp.broadcast_to(slot_ref[...], (experts, experts))
        ).astype(F32).astype(BF16)
        best = lax.fori_loop(0, depth, up_max, jnp.zeros((experts, 2 * half), BF16))
        up = jnp.dot(choose, best, preferred_element_type=F32)
        load_d.wait()
        best = lax.fori_loop(0, fl, down_max, jnp.zeros((experts, width), BF16))
        down = jnp.dot(choose, best, preferred_element_type=F32)
        for slot in range(experts):
            s_send[slot, :, pl.ds(0, 2 * half)] = up[slot : slot + 1]
            s_send[slot, :, pl.ds(2 * half, width)] = down[slot : slot + 1]
        s_recv[me] = s_send[me]

    load_w.wait()
    tile = 2 * depth

    @pl.loop(0, w_ref.shape[1] // tile)
    def _(c):
        cols = pl.ds(pl.multiple_of(c * tile, tile), tile)

        @pl.loop(0, w_ref.shape[0] // tile)
        def _(r):
            rows = pl.ds(pl.multiple_of(r * tile, tile), tile)
            wt_ref[cols, rows] = w_ref[rows, cols].T

    scales_in()
    for i in range(1, n):
        meta_copy(i).wait_recv()
        tok_copy(i).wait_recv()

    row = lax.broadcasted_iota(jnp.int32, (total, total), 0)
    col = lax.broadcasted_iota(jnp.int32, (total, total), 1)
    source = (lax.rem(row, span) // small) * own + (row // span) * small + lax.rem(row, small)
    order = (source == col).astype(F32).astype(BF16)
    tok_p = jnp.dot(order, tok_all[...], preferred_element_type=F32).T
    meta_p = jnp.dot(order, meta_all[...], preferred_element_type=F32).T
    gate_p = meta_p[top : 2 * top] + meta_p[2 * top : 3 * top] + meta_p[3 * top : 4 * top]
    for g in range(groups):
        lo, hi = g * span, (g + 1) * span
        for c in range(copies):
            tok_t[g, :, c * span : (c + 1) * span] = tok_p[:, lo:hi]
            for chunk in range(per):
                k, at = chunk * copies + c, g * per + chunk
                id_row[at : at + 1, c * span : (c + 1) * span] = meta_p[k : k + 1, lo:hi]
                gate_row[at : at + 1, c * span : (c + 1) * span] = gate_p[k : k + 1, lo:hi]

    lanes = lax.broadcasted_iota(jnp.int32, (experts, total), 0).astype(F32)

    def mask_of(k):
        return id_row[pl.ds(k, 1), :] == lanes

    def partner(s):
        bit = 1 << s
        return me + bit * (1 - 2 * lax.rem(me // bit, 2))

    def h_copy(k, s):
        return remote(hs[s].at[k], hr[s].at[k], h_ssem.at[s, k], h_rsem.at[s, k], partner(s))

    def o_copy(q, s):
        return remote(os_[s].at[q], or_[s].at[q], o_ssem.at[s, q], o_rsem.at[s, q], partner(s))

    def h_rows(k, j, part):
        return h_ref[k, pl.ds(pl.multiple_of(part * half + j * fl, 16), fl), :]

    def h_sum(k, j, s, part):
        total_ = h_rows(k, j, part)
        for prior in range(s):
            total_ += hr[prior][k, j // (2 << prior), pl.ds(part * fl, fl), :].astype(F32)
        return total_

    def product(k):
        mask = mask_of(k)

        @pl.loop(0, depth // 8)
        def _(block):
            for inner in range(8):
                d = block * 8 + inner
                row = jnp.where(mask, tok_t[k // per, pl.ds(d, 1), :], 0.0)
                x_ref[pl.ds(pl.multiple_of(d * experts, experts), experts), :] = row.astype(BF16)

        h_ref[k] = jnp.dot(wt_ref[...], x_ref[...], preferred_element_type=F32)

    def h_send(k, s):
        if s > 0:
            h_copy(k, s - 1).wait_recv()
        bit = 1 << s
        base = (1 - lax.rem(me // bit, 2)) * bit + lax.rem(me, bit)
        for m in range(n // (2 * bit)):
            j = m * 2 * bit + base
            for part in range(2):
                hs[s][k, m, pl.ds(part * fl, fl), :] = h_sum(k, j, s, part).astype(hs[s].dtype)
        h_copy(k, s).start()

    def h_final(k):
        h_copy(k, bits - 1).wait_recv()
        gate = h_sum(k, me, bits, 0)
        act = gate / (1.0 + jnp.exp(-gate)) * h_sum(k, me, bits, 1)
        act_ref[...] = act * gate_row[pl.ds(k, 1), :]
        mask = mask_of(k)

        @pl.loop(0, fl // 8)
        def _(block):
            for inner in range(8):
                f = block * 8 + inner
                rows = pl.ds(pl.multiple_of(f * experts, experts), experts)
                placed = jnp.where(mask, act_ref[pl.ds(f, 1), :], 0.0)
                for c in range(copies):
                    a_ref[k // per, rows, :] += placed[:, c * span : (c + 1) * span]

    def o_sum(g, j, s):
        total_ = o_ref[g, pl.ds(pl.multiple_of(j * small, small), small), :]
        for prior in range(s):
            total_ += or_[prior][g, j // (2 << prior)].astype(F32)
        return total_

    def o_product(g):
        a_t = a_ref[g].T.astype(BF16)
        wide = width // 4

        @pl.loop(0, 4)
        def _(c):
            cols = pl.ds(pl.multiple_of(c * wide, wide), wide)
            o_ref[g, :, cols] = jnp.dot(a_t, d_ref[:, cols], preferred_element_type=F32)

    def o_send(g, s):
        if s > 0:
            o_copy(g, s - 1).wait_recv()
        bit = 1 << s
        base = (1 - lax.rem(me // bit, 2)) * bit + lax.rem(me, bit)
        for m in range(n // (2 * bit)):
            os_[s][g, m] = o_sum(g, m * 2 * bit + base, s).astype(os_[s].dtype)
        o_copy(g, s).start()

    def o_final(g):
        o_copy(g, bits - 1).wait_recv()
        out32[pl.ds(pl.multiple_of(g * small, small), small), :] = o_sum(g, me, bits)

    lags = [s + (s > 1) for s in range(bits + 1)]
    late = lags[bits]
    lead = per - 1 + late

    @pl.loop(0, (groups - 1) * per + lead + late + 1)
    def _(step):
        @pl.when(step < chunks)
        def _():
            product(step)
            h_send(step, 0)

        for s in range(1, bits):
            @pl.when((step >= lags[s]) & (step < chunks + lags[s]))
            def _():
                h_send(step - lags[s], s)

        @pl.when((step >= late) & (step < chunks + late))
        def _():
            h_final(step - late)

        for s in range(bits + 1):
            since = step - lead - lags[s]

            @pl.when((since >= 0) & (lax.rem(since + per * (late + chunks), per) == 0) & (since < chunks))
            def _():
                g = since // per
                if s == 0:
                    o_product(g)
                if s < bits:
                    o_send(g, s)
                else:
                    o_final(g)

        @pl.when(step == 1)
        def _():
            for i in range(1, n):
                scale_copy(i).start()

    out_ref[...] = out32[...].astype(BF16)
    for i in range(1, n):
        scale_copy(i).wait_recv()
    best = s_recv[0]
    for i in range(1, n):
        best = jnp.maximum(best, s_recv[i])
    scale_ref[:, pl.ds(0, 2 * half)] = best[:, : 2 * half] * root_d
    scale_ref[:, pl.ds(2 * half, width)] = best[:, 2 * half :] * root_f
    for i in range(1, n):
        meta_copy(i).wait_send()
        tok_copy(i).wait_send()
        scale_copy(i).wait_send()

    @pl.loop(0, chunks)
    def _(k):
        for s in range(bits):
            h_copy(k, s).wait_send()

    for g in range(groups):
        for s in range(bits):
            o_copy(g, s).wait_send()


def fused(tokens, gate_up, down_proj, expert_ids, gate_weights, owner_slot):
    n = lax.axis_size("ep")
    bits = n.bit_length() - 1
    own, width = tokens.shape
    depth, experts, both = gate_up.shape
    fl = down_proj.shape[0]
    top = expert_ids.shape[1]
    total = own * n
    groups = 2
    chunks = top
    span = total // groups
    vmem = pl.BlockSpec(memory_space=pltpu.VMEM)
    hbm = pl.BlockSpec(memory_space=pl.ANY)
    counts = [n >> (s + 1) for s in range(bits)]
    kinds = [BF16 if s else F32 for s in range(bits)]
    hidden_bufs = [pltpu.VMEM((chunks, c, 2 * fl, total), t) for c, t in zip(counts, kinds)]
    out_bufs = [pltpu.VMEM((groups, c, own // groups, width), t) for c, t in zip(counts, kinds)]
    return pl.pallas_call(
        functools.partial(fused_kernel, (n, bits, chunks, groups)),
        out_shape=(
            jax.ShapeDtypeStruct((own, width), BF16),
            jax.ShapeDtypeStruct((1, both + width), F32),
        ),
        in_specs=[vmem, vmem, vmem, vmem, hbm, hbm],
        out_specs=(vmem, vmem),
        scratch_shapes=[
            pltpu.VMEM((depth * experts, both), BF16),
            pltpu.VMEM((both, depth * experts), BF16),
            pltpu.VMEM((fl * experts, width), BF16),
            pltpu.VMEM((own, 128), F32),
            pltpu.VMEM((own, 128), BF16),
            pltpu.VMEM((total, depth), BF16),
            pltpu.VMEM((groups, depth, total), F32),
            pltpu.VMEM((total, 128), BF16),
            pltpu.VMEM((chunks, total), F32),
            pltpu.VMEM((chunks, total), F32),
            pltpu.VMEM((depth * experts, total), BF16),
            pltpu.VMEM((chunks, both, total), F32),
            pltpu.VMEM((fl, total), F32),
            pltpu.VMEM((groups, fl * experts, span), F32),
            pltpu.VMEM((groups, span, width), F32),
            pltpu.VMEM((own, width), F32),
            pltpu.VMEM((n, 1, both + width), F32),
            pltpu.VMEM((n, 1, both + width), F32),
            *hidden_bufs, *hidden_bufs, *out_bufs, *out_bufs,
            pltpu.SemaphoreType.DMA((2,)),
            pltpu.SemaphoreType.DMA((3, n)),
            pltpu.SemaphoreType.DMA((3, n)),
            pltpu.SemaphoreType.DMA((bits, chunks)),
            pltpu.SemaphoreType.DMA((bits, chunks)),
            pltpu.SemaphoreType.DMA((bits, groups)),
            pltpu.SemaphoreType.DMA((bits, groups)),
        ],
        compiler_params=pltpu.CompilerParams(
            collective_id=0, has_side_effects=True, vmem_limit_bytes=60 * 2**20
        ),
    )(
        tokens,
        expert_ids,
        gate_weights,
        owner_slot.reshape(1, experts),
        gate_up.reshape(depth * experts, both),
        down_proj.reshape(fl * experts, width),
    )


def layer(tokens, gate_up, down_proj, expert_ids, gate_weights, owner_slot):
    n = lax.axis_size("ep")
    own = tokens.shape[0]
    depth, experts, both = gate_up.shape
    partials = n * own * expert_ids.shape[1] * both
    aligned = (
        n & (n - 1) == 0 and depth % 128 == 0 and experts == n and experts % 16 == 0
        and down_proj.shape[0] % 16 == 0 and own % 16 == 0
    )
    args = (tokens, gate_up, down_proj, expert_ids, gate_weights, owner_slot)
    return fused(*args) if aligned and partials <= gate_up.size else shards(*args)


def solution(mesh):
    in_specs = (
        P(("parts", "ep"), None),
        P(("parts", "ep"), None, None),
        P(("parts", "ep"), None, None),
        P(("parts", "ep"), None),
        P(("parts", "ep"), None),
        P("parts"),
    )
    out_specs = (P(("parts", "ep"), None), P(("parts", "ep"), None))
    return jax.shard_map(layer, mesh=mesh, in_specs=in_specs, out_specs=out_specs, check_vma=False)
```

profile of v0, /device:TPU:0, one launch (start us, length us, event | category | flops | bytes accessed | tf_op | source)
XLA Modules:
  0.0 87.0 jit_solution(2042268235297125886)
XLA Ops:
  0.6 1.4 %copy.8.ids_ref = s32[16,8]{1,0:T(8,128)} copy(s32[16,8]{0,1:T(8,128)} %param.9) | data formatting | bytes 1024 | tf_op args[3]
  2.0 1.4 %copy.9.gate_ref = f32[16,8]{1,0:T(8,128)} copy(f32[16,8]{0,1:T(8,128)} %param.10) | data formatting | bytes 1024 | tf_op args[4]
  3.3 80.9 %shard_map.77 = (bf16[16,2048]{1,0:T(8,128)(2,1)}, f32[1,3584]{1,0:T(1,128)}) custom-call(bf16[16,2048]{1,0:T(8,128)(2,1)} %tok_ref.1, s32[16,8]{1,0:T(8,128)} %copy.8.ids_ref, f32[16,8]{1,0:T(8,128)} %copy.9.gate_ref, s32[1,16]{1,0:T(1,128)} %bitcast.5, bf16[2048,1536]{1,0:T(8,128)(2,1)} %bitcast.3, bf16[768,2048]{1,0:T(8,128)(2,1)} %bitcast.4), custom_call_target="tpu_custom_call" | custom-call | tf_op jit(solution)/shard_map/pallas_call | solution.py:375
  84.2 1.5 %copy.12 = bf16[16,2048]{1,0:T(8,128)(2,1)} copy(bf16[16,2048]{1,0:T(8,128)(2,1)} %get-tuple-element.4) | data formatting | bytes 131072
  85.7 1.3 %copy.13 = f32[1,3584]{1,0:T(1,128)} copy(f32[1,3584]{1,0:T(1,128)} %get-tuple-element.5) | data formatting | bytes 28672
where the time goes:
time: 87.3 us; the launch traced here: 87 us
  Pallas kernels  80.9 us (93%)
  local copies, waits for them, and re-layouts  5.5 us (6%)
    pallas_call x1, Pallas kernels, fused(): pl.pallas_call(functools.partial(fused_kernel, (n, bits, chunks, groups))...  80.9 us
    unnamed x4, local copies, waits for them, and re-layouts  5.5 us

commit v1 on v0

v1 whole, which is shorter than its diff:
```python
import functools
import math

import jax
import jax.numpy as jnp
from jax import lax
from jax.experimental import pallas as pl
from jax.experimental.pallas import tpu as pltpu
from jax.sharding import PartitionSpec as P


def expert_block(arrived, held_up, held_down):
    hidden = jnp.einsum("rjd,djf->rjf", arrived, held_up, preferred_element_type=jnp.float32)
    ffn_width = held_up.shape[2] // 2
    activated = (jax.nn.silu(hidden[..., :ffn_width]) * hidden[..., ffn_width:]).astype(
        jnp.bfloat16
    )
    return jnp.einsum(
        "rjf,fjd->rjd", activated, held_down, preferred_element_type=jnp.float32
    ).astype(jnp.bfloat16)


def column_scales(gate_up, down_proj):
    gate_scale = jnp.max(jnp.abs(gate_up), axis=0).astype(jnp.float32) * math.sqrt(gate_up.shape[0])
    down_scale = jnp.max(jnp.abs(down_proj), axis=0).astype(jnp.float32) * math.sqrt(
        down_proj.shape[0]
    )
    return jnp.concatenate([gate_scale, down_scale], axis=1)


def shards(tokens, gate_up, down_proj, expert_ids, gate_weights, owner_slot):
    tok_rows, model_width = tokens.shape
    top_count = expert_ids.shape[1]
    slots_all = gate_up.shape[1]
    devices = lax.axis_size("ep")
    own_count = slots_all // devices
    capacity = 2 * tok_rows * top_count // slots_all
    experts_iota = jnp.arange(slots_all, dtype=jnp.int32)
    inverse = jnp.zeros((slots_all,), jnp.int32).at[owner_slot].set(experts_iota)
    flat_ids = expert_ids.reshape(-1)
    one_hot = (flat_ids[:, None] == experts_iota[None, :]).astype(jnp.int32)
    slot_rank = jnp.sum((jnp.cumsum(one_hot, axis=0) - 1) * one_hot, axis=1)
    position = slot_rank * slots_all + flat_ids
    source_rows = jnp.repeat(tokens, top_count, axis=0)
    outbox = (
        jnp.zeros((capacity * slots_all, model_width), jnp.bfloat16).at[position].set(source_rows)
    )
    outbox = outbox.reshape(capacity, slots_all, model_width)
    held_up, held_down = (
        lax.all_to_all(gate_up, "ep", split_axis=1, concat_axis=0, tiled=True),
        lax.all_to_all(down_proj, "ep", split_axis=1, concat_axis=0, tiled=True),
    )
    arrived = lax.all_to_all(outbox, "ep", split_axis=1, concat_axis=0, tiled=True)
    expert_out = expert_block(arrived, held_up, held_down)
    returned = lax.all_to_all(expert_out, "ep", split_axis=0, concat_axis=1, tiled=True).reshape(
        capacity * slots_all, model_width
    )
    picked = returned[position].astype(jnp.float32).reshape(tok_rows, top_count, model_width)
    moe_out = jnp.sum(picked * gate_weights[:, :, None], axis=1).astype(jnp.bfloat16)
    scales = column_scales(held_up, held_down)
    every_row = lax.all_gather(scales, "ep", axis=0, tiled=True)
    mine = lax.dynamic_slice_in_dim(inverse, lax.axis_index("ep") * own_count, own_count)
    scales = jnp.take(every_row, mine, axis=0)
    return (moe_out, scales)


MESH = pl.DeviceIdType.MESH
F32, BF16 = jnp.float32, jnp.bfloat16
GROUPS = 4
LATERAL = 1


def orders(bits):
    across = tuple(range(bits))
    return across, across[1:] + across[:1]


def fused_kernel(
    dims, tok_ref, ids_ref, gate_ref, slot_ref, up_hbm, down_hbm, out_ref, scale_ref,
    w_ref, wt_ref, wt_in, d_ref, parcel, tok_all, turned_ref, tok_t, gates_ref, pat_ref, x_ref,
    h_ref, act_ref, spread_ref, o_ref, o_in, out32, s_pair, s_send, s_recv, *rest,
):
    m, bits = dims
    hs, hr = rest[:bits], rest[bits : 2 * bits]
    (
        os_, or_, w_sem, d_sem, wt_ssem, wt_rsem, tok_ssem, tok_rsem, scale_ssem, scale_rsem,
        pair_ssem, pair_rsem, h_ssem, h_rsem, p_ssem, p_rsem, o_ssem, o_rsem,
    ) = rest[2 * bits :]
    n = 2 * m
    me = lax.axis_index("ep")
    chip, core = me // 2, lax.rem(me, 2)
    own = tok_ref.shape[0]
    total = tok_all.shape[0]
    deep = x_ref.shape[0] * x_ref.shape[1] // slot_ref.shape[1]
    depth = deep // 2
    experts = slot_ref.shape[1]
    top = ids_ref.shape[0]
    groups, small = GROUPS, own // GROUPS
    span = m * small
    lanes = span * top
    pieces = 2 * groups
    half = w_ref.shape[1] // 2
    fl = half // n
    width = d_ref.shape[1]
    root_d, root_f = math.sqrt(deep * m), math.sqrt(half)
    tile = 256
    blocks = w_ref.shape[0] // tile

    def load_w(r):
        rows = pl.ds(pl.multiple_of(r * tile, tile), tile)
        return pltpu.make_async_copy(up_hbm.at[rows, :], w_ref.at[rows, :], w_sem.at[r])

    load_d = pltpu.make_async_copy(down_hbm, d_ref, d_sem.at[0])
    for r in range(blocks):
        load_w(r).start()
    load_d.start()

    def remote(src, dst, ssem, rsem, peer):
        return pltpu.make_async_remote_copy(
            src_ref=src, dst_ref=dst, send_sem=ssem, recv_sem=rsem,
            device_id={"ep": peer}, device_id_type=MESH,
        )

    mate = 2 * chip + 1 - core

    def across(i):
        return lax.rem(chip + i, m)

    barrier = pltpu.get_barrier_semaphore()
    for i in range(1, n):
        pl.semaphore_signal(
            barrier, inc=1, device_id={"ep": lax.rem(me + i, n)}, device_id_type=MESH
        )

    gates = gate_ref[...]
    facts = [ids_ref[...].astype(F32)]
    for _ in range(3):
        high = gates.astype(BF16).astype(F32)
        facts.append(high)
        gates = gates - high
    facts.append(jnp.zeros((128 - 4 * top, own), F32))
    same = (
        lax.broadcasted_iota(jnp.int32, (own, own), 0)
        == lax.broadcasted_iota(jnp.int32, (own, own), 1)
    ).astype(F32).astype(BF16)
    meta = lax.dot_general(
        same, jnp.concatenate(facts, axis=0).astype(BF16), (((1,), (1,)), ((), ())),
        preferred_element_type=F32,
    ).astype(BF16)
    for j in range(m):
        parcel[j, :, 0:deep] = tok_ref[:, j * deep : (j + 1) * deep]
        parcel[j, :, deep : deep + 128] = meta
    pl.semaphore_wait(barrier, n - 1)

    mine = pl.ds(pl.multiple_of(me * own, own), own)

    def tok_copy(i):
        peer = lax.rem(me + i, n)
        return remote(
            parcel.at[peer // 2], tok_all.at[mine, :], tok_ssem.at[i], tok_rsem.at[i], peer
        )

    def scale_copy(i):
        to = 2 * across(i) + core
        return remote(s_send.at[to], s_recv.at[chip], scale_ssem.at[i], scale_rsem.at[i], to)

    def wt_copy(r):
        at = pl.ds(pl.multiple_of(r * tile, tile), tile)
        return remote(
            wt_ref.at[1 - core, :, at], wt_in.at[:, at], wt_ssem.at[r], wt_rsem.at[r], mate
        )

    pair_copy = remote(s_pair.at[0], s_pair.at[1], pair_ssem.at[0], pair_rsem.at[0], mate)

    for i in range(1, n):
        tok_copy(i).start()
    tok_all[mine, :] = parcel[chip]

    @pl.loop(0, blocks)
    def _(r):
        load_w(r).wait()
        rows = pl.ds(pl.multiple_of(r * tile, tile), tile)
        for at in range(0, 2 * half, tile):
            turned = w_ref[rows, at : at + tile].T
            part, first = at // half, at % half
            done = 0
            while done < tile:
                device, f = (first + done) // fl, (first + done) % fl
                count = min(fl - f, tile - done)
                to = (device // 2) * 2 * fl + part * fl + f
                wt_ref[device % 2, to : to + count, rows] = turned[done : done + count]
                done += count
        wt_copy(r).start()

    act_ref[...] = jnp.zeros_like(act_ref)
    spread_ref[...] = (
        lax.broadcasted_iota(jnp.int32, spread_ref.shape, 0)
        == lax.broadcasted_iota(jnp.int32, spread_ref.shape, 1) // experts
    ).astype(F32).astype(BF16)
    for i in range(1, n):
        tok_copy(i).wait_recv()
    turned_ref[...] = tok_all[...].T
    load_d.wait()

    def peer_of(bit):
        step = 1 << bit
        return 2 * (chip + step * (1 - 2 * lax.rem(chip // step, 2))) + core

    def h_copy(q, s, order):
        return remote(
            hs[s].at[q], hr[s].at[q], h_ssem.at[s, q], h_rsem.at[s, q], peer_of(order[s])
        )

    def h_rows(q, j, part):
        at = pl.multiple_of(j * 2 * fl + part * fl, 16)
        return h_ref[q, pl.ds(at, fl), :]

    def h_sum(q, j, s, part, order):
        total_ = h_rows(q, j, part)
        for prior in range(s):
            at = 0
            for i, bit in enumerate(sorted(order[prior + 1 :])):
                at = at + (lax.rem(j // (1 << bit), 2) << i)
            total_ += hr[prior][q, at, pl.ds(part * fl, fl), :].astype(F32)
        return total_

    def h_send(q, s, order):
        if s > 0:
            h_copy(q, s - 1, order).wait_recv()
        base = (1 - lax.rem(chip // (1 << order[s]), 2)) * (1 << order[s])
        for bit in order[:s]:
            base = base + lax.rem(chip // (1 << bit), 2) * (1 << bit)
        left = sorted(order[s + 1 :])
        for at in range(1 << len(left)):
            j = base + sum(((at >> i) & 1) << bit for i, bit in enumerate(left))
            for part in range(2):
                hs[s][q, at, pl.ds(part * fl, fl), :] = h_sum(q, j, s, part, order).astype(BF16)
        h_copy(q, s, order).start()

    def either(q, run):
        usual, lateral = orders(bits)

        @pl.when(q == LATERAL)
        def _():
            run(lateral)

        @pl.when(q != LATERAL)
        def _():
            run(usual)

    def product(q):
        p, g = lax.rem(q, 2), q // 2
        lane = lax.broadcasted_iota(jnp.int32, (1, lanes), 1)
        spot = lax.rem(lane, span)
        source = (2 * (spot // small) + p) * own + g * small + lax.rem(spot, small)
        pick = (
            lax.broadcasted_iota(jnp.int32, (total, lanes), 0) == source
        ).astype(F32).astype(BF16)
        in_slot = lax.broadcasted_iota(jnp.int32, (top, lanes), 0) == lane // span
        picked = jnp.dot(turned_ref[...], pick, preferred_element_type=F32)
        tok_t[...] = picked[0:deep]
        facts = picked[deep : deep + 4 * top]
        gate_sum = facts[top : 2 * top] + facts[2 * top : 3 * top] + facts[3 * top : 4 * top]
        ids = jnp.sum(jnp.where(in_slot, facts[0:top], 0.0), axis=0, keepdims=True)
        gates_ref[q] = jnp.sum(jnp.where(in_slot, gate_sum, 0.0), axis=0, keepdims=True)
        mask = ids == lax.broadcasted_iota(jnp.int32, (experts, lanes), 0).astype(F32)
        wide = jnp.broadcast_to(ids, (128, lanes)).T
        marks = lax.rem(lax.broadcasted_iota(jnp.int32, (lanes, 128), 1), experts).astype(F32)
        pat_ref[q] = (wide == marks).astype(F32)

        @pl.loop(0, depth // 8)
        def _(block):
            for side in range(2):
                for inner in range(8):
                    d = block * 8 + inner
                    row = jnp.where(mask, tok_t[pl.ds(side * depth + d, 1), :], 0.0)
                    at = pl.ds(pl.multiple_of(d * experts, experts), experts)
                    x_ref[side, at, :] = row.astype(BF16)


        h_ref[q] = jnp.dot(
            wt_ref[core], x_ref[core], preferred_element_type=F32
        ) + jnp.dot(wt_in[...], x_ref[1 - core], preferred_element_type=F32)

    def p_copy(q):
        return remote(o_ref.at[q], o_in.at[q // 2], p_ssem.at[q // 2], p_rsem.at[q // 2], mate)

    def o_copy(g, i):
        peer = across(i)
        return remote(
            os_.at[g, peer], or_.at[g, chip], o_ssem.at[g, i], o_rsem.at[g, i], 2 * peer + core
        )

    def h_final(q, order):
        h_copy(q, bits - 1, order).wait_recv()
        gate = h_sum(q, chip, bits, 0, order)
        act = gate / (1.0 + jnp.exp(-gate)) * h_sum(q, chip, bits, 1, order)
        act_ref[0:fl, :] = act * gates_ref[q]

    def o_product(q):
        spread = jnp.dot(
            act_ref[...].T.astype(BF16), spread_ref[...], preferred_element_type=F32
        )
        folded = []
        for at in range(0, fl * experts, 128):
            sum_ = spread[0:span, at : at + 128] * pat_ref[q, 0:span]
            for k in range(1, top):
                rows = slice(k * span, (k + 1) * span)
                sum_ += spread[rows, at : at + 128] * pat_ref[q, rows]
            folded.append(sum_.astype(BF16))
        placed = jnp.concatenate(folded, axis=1)
        o_ref[q] = jnp.dot(placed, d_ref[...], preferred_element_type=F32)

        @pl.when(core != lax.rem(q, 2))
        def _():
            p_copy(q).start()

    def o_send(q):
        g = q // 2

        @pl.when(core == lax.rem(q, 2))
        def _():
            p_copy(q).wait_recv()
            both = o_ref[q] + o_in[g]
            for j in range(m):
                os_[g, j] = both[j * small : (j + 1) * small].astype(BF16)
            for i in range(1, m):
                o_copy(g, i).start()

    def o_final(q):
        g = q // 2

        @pl.when(core == lax.rem(q, 2))
        def _():
            for i in range(1, m):
                o_copy(g, i).wait_recv()
            total_ = os_[g, chip].astype(F32)
            for i in range(1, m):
                total_ += or_[g, across(i)].astype(F32)
            out32[g] = total_

    def scales_in():
        def up_max(r, best):
            rows = pl.ds(pl.multiple_of(r * experts, experts), experts)
            return jnp.maximum(best, jnp.abs(w_ref[rows, :]))

        def down_max(r, best):
            rows = pl.ds(pl.multiple_of(r * experts, experts), experts)
            return jnp.maximum(best, jnp.abs(d_ref[rows, :]))

        choose = (
            lax.broadcasted_iota(jnp.int32, (experts, experts), 0)
            == jnp.broadcast_to(slot_ref[...], (experts, experts))
        ).astype(F32).astype(BF16)
        best = lax.fori_loop(0, depth, up_max, jnp.zeros((experts, 2 * half), BF16))
        s_pair[0, :, pl.ds(0, 2 * half)] = jnp.dot(
            choose, best, preferred_element_type=F32
        ).astype(BF16)
        best = lax.fori_loop(0, fl, down_max, jnp.zeros((experts, width), BF16))
        s_pair[0, :, pl.ds(2 * half, width)] = jnp.dot(
            choose, best, preferred_element_type=F32
        ).astype(BF16)
        pair_copy.start()

    def scales_out():
        pair_copy.wait_recv()
        best = jnp.maximum(s_pair[0].astype(F32), s_pair[1].astype(F32))
        for slot in range(experts):
            s_send[slot] = best[slot : slot + 1]
        for i in range(1, m):
            scale_copy(i).start()

    for r in range(blocks):
        wt_copy(r).wait_recv()
    lags = [0] + [s + 1 for s in range(1, bits + 1)]
    late = lags[bits]

    @pl.loop(0, pieces + late + 2)
    def _(step):
        @pl.when(step < pieces)
        def _():
            product(step)
            either(step, functools.partial(h_send, step, 0))

        for s in range(1, bits):
            @pl.when((step >= lags[s]) & (step < pieces + lags[s]))
            def _():
                either(step - lags[s], functools.partial(h_send, step - lags[s], s))

        @pl.when((step >= late) & (step < pieces + late))
        def _():
            either(step - late, functools.partial(h_final, step - late))
            o_product(step - late)

        @pl.when((step >= late + 1) & (step < pieces + late + 1))
        def _():
            o_send(step - late - 1)

        @pl.when(step >= late + 2)
        def _():
            o_final(step - late - 2)

        @pl.when(step == pieces)
        def _():
            scales_in()

        @pl.when(step == pieces + 1)
        def _():
            scales_out()

    out_ref[...] = jnp.concatenate([out32[g] for g in range(groups)], axis=0).astype(BF16)
    for i in range(1, m):
        scale_copy(i).wait_recv()
    best = s_send[me]
    for i in range(1, m):
        best = jnp.maximum(best, s_recv[across(i)])
    scale_ref[:, pl.ds(0, 2 * half)] = best[:, : 2 * half] * root_d
    scale_ref[:, pl.ds(2 * half, width)] = best[:, 2 * half :] * root_f
    for i in range(1, n):
        tok_copy(i).wait_send()
    for i in range(1, m):
        scale_copy(i).wait_send()
    for r in range(blocks):
        wt_copy(r).wait_send()
    pair_copy.wait_send()

    @pl.loop(0, pieces)
    def _(q):
        for s in range(bits):
            h_copy(q, s, orders(bits)[0]).wait_send()

    @pl.loop(0, groups)
    def _(g):
        p_copy(2 * g + 1 - core).wait_send()
        for i in range(1, m):
            o_copy(g, i).wait_send()


def fused(tokens, gate_up, down_proj, expert_ids, gate_weights, owner_slot):
    m = lax.axis_size("ep") // 2
    bits = m.bit_length() - 1
    own, width = tokens.shape
    depth, experts, both = gate_up.shape
    fl = down_proj.shape[0]
    top = expert_ids.shape[1]
    total = own * 2 * m
    small = own // GROUPS
    span = m * small
    lanes = span * top
    pieces = 2 * GROUPS
    blocks = depth * experts // 256
    vmem = pl.BlockSpec(memory_space=pltpu.VMEM)
    hbm = pl.BlockSpec(memory_space=pl.ANY)
    bufs = [pltpu.VMEM((pieces, m >> (s + 1), 2 * fl, lanes), BF16) for s in range(bits)]
    dma = pltpu.SemaphoreType.DMA
    return pl.pallas_call(
        functools.partial(fused_kernel, (m, bits)),
        out_shape=(
            jax.ShapeDtypeStruct((own, width), BF16),
            jax.ShapeDtypeStruct((1, both + width), F32),
        ),
        in_specs=[vmem, vmem, vmem, vmem, hbm, hbm],
        out_specs=(vmem, vmem),
        scratch_shapes=[
            pltpu.VMEM((depth * experts, both), BF16),
            pltpu.VMEM((2, both // 2, depth * experts), BF16),
            pltpu.VMEM((both // 2, depth * experts), BF16),
            pltpu.VMEM((fl * experts, width), BF16),
            pltpu.VMEM((m, own, 2 * depth + 128), BF16),
            pltpu.VMEM((total, 2 * depth + 128), BF16),
            pltpu.VMEM((2 * depth + 128, total), BF16),
            pltpu.VMEM((2 * depth, lanes), F32),
            pltpu.VMEM((pieces, 1, lanes), F32),
            pltpu.VMEM((pieces, lanes, 128), F32),
            pltpu.VMEM((2, depth * experts, lanes), BF16),
            pltpu.VMEM((pieces, both // 2, lanes), F32),
            pltpu.VMEM((128, lanes), F32),
            pltpu.VMEM((128, fl * experts), BF16),
            pltpu.VMEM((pieces, span, width), F32),
            pltpu.VMEM((GROUPS, span, width), F32),
            pltpu.VMEM((GROUPS, small, width), F32),
            pltpu.VMEM((2, experts, both + width), BF16),
            pltpu.VMEM((experts, 1, both + width), F32),
            pltpu.VMEM((m, 1, both + width), F32),
            *bufs, *bufs,
            pltpu.VMEM((GROUPS, m, small, width), BF16),
            pltpu.VMEM((GROUPS, m, small, width), BF16),
            dma((blocks,)), dma((1,)), dma((blocks,)), dma((blocks,)),
            dma((2 * m,)), dma((2 * m,)), dma((m,)), dma((m,)), dma((1,)), dma((1,)),
            dma((bits, pieces)), dma((bits, pieces)), dma((GROUPS,)), dma((GROUPS,)),
            dma((GROUPS, m)), dma((GROUPS, m)),
        ],
        compiler_params=pltpu.CompilerParams(
            collective_id=0, has_side_effects=True, vmem_limit_bytes=60 * 2**20
        ),
    )(
        tokens,
        expert_ids.T,
        gate_weights.T,
        owner_slot.reshape(1, experts),
        gate_up.reshape(depth * experts, both),
        down_proj.reshape(fl * experts, width),
    )


def layer(tokens, gate_up, down_proj, expert_ids, gate_weights, owner_slot):
    n = lax.axis_size("ep")
    own = tokens.shape[0]
    depth, experts, both = gate_up.shape
    partials = n * own * expert_ids.shape[1] * both
    aligned = (
        n & (n - 1) == 0 and depth % 128 == 0 and experts == n and experts % 16 == 0
        and down_proj.shape[0] % 16 == 0 and down_proj.shape[0] <= 128 and own % 16 == 0
        and n >= 4 and n * own * expert_ids.shape[1] % (256 * GROUPS) == 0
    )
    args = (tokens, gate_up, down_proj, expert_ids, gate_weights, owner_slot)
    return fused(*args) if aligned and partials <= gate_up.size else shards(*args)


def solution(mesh):
    in_specs = (
        P(("parts", "ep"), None),
        P(("parts", "ep"), None, None),
        P(("parts", "ep"), None, None),
        P(("parts", "ep"), None),
        P(("parts", "ep"), None),
        P("parts"),
    )
    out_specs = (P(("parts", "ep"), None), P(("parts", "ep"), None))
    return jax.shard_map(layer, mesh=mesh, in_specs=in_specs, out_specs=out_specs, check_vma=False)
```

time: 87.3 us -> 80.8 us (0.926)
  Pallas kernels: 80.9 us -> 76.9 us
  local copies, waits for them, and re-layouts: 5.5 us -> 2.79 us
    pallas_call x1, Pallas kernels: 80.9 us -> 76.9 us  [fused(): pl.pallas_call(functools.partial(fused_kernel, (m, bits)), out_shape=(jax...]
    unnamed x4 -> x2, local copies, waits for them, and re-layouts: 5.5 us -> 2.79 us
where the time goes in v1:
time: 80.8 us; the launch traced here: 80.3 us
  Pallas kernels  76.9 us (95%)
  local copies, waits for them, and re-layouts  2.79 us (3%)
    pallas_call x1, Pallas kernels, fused(): pl.pallas_call(functools.partial(fused_kernel, (m, bits)), out_shape=(jax...  76.9 us
    unnamed x2, local copies, waits for them, and re-layouts  2.79 us

profile of v1, /device:TPU:0, one launch (start us, length us, event | category | flops | bytes accessed | tf_op | source)
XLA Modules:
  0.0 80.3 jit_solution(12436722158985159427)
XLA Ops:
  0.6 76.9 %shard_map.77 = (bf16[16,2048]{1,0:T(8,128)(2,1)}, f32[1,3584]{1,0:T(1,128)}) custom-call(bf16[16,2048]{1,0:T(8,128)(2,1)} %tok_ref.1, s32[8,16]{1,0:T(8,128)} %bitcast.7, f32[8,16]{1,0:T(8,128)} %bitcast.8, s32[1,16]{1,0:T(1,128)} %bitcast.9, bf16[2048,1536]{1,0:T(8,128)(2,1)} %bitcast.5, bf16[768,2048]{1,0:T(8,128)(2,1)} %bitcast.6), custom_call_target="tpu_custom_call" | custom-call | tf_op jit(solution)/shard_map/pallas_call | solution.py:456
  77.5 1.5 %copy.10 = bf16[16,2048]{1,0:T(8,128)(2,1)} copy(bf16[16,2048]{1,0:T(8,128)(2,1)} %get-tuple-element.4) | data formatting | bytes 131072
  79.0 1.3 %copy.11 = f32[1,3584]{1,0:T(1,128)} copy(f32[1,3584]{1,0:T(1,128)} %get-tuple-element.5) | data formatting | bytes 28672

commit v2 on v1

--- a/solution.py
+++ b/solution.py
@@ -67,7 +67,7 @@
 MESH = pl.DeviceIdType.MESH
 F32, BF16 = jnp.float32, jnp.bfloat16
 GROUPS = 4
-LATERAL = 1
+LATERAL = 2
 
 
 def orders(bits):
@@ -176,8 +176,13 @@
         tok_copy(i).start()
     tok_all[mine, :] = parcel[chip]
 
-    @pl.loop(0, blocks)
-    def _(r):
+    def largest(ref, first, count, best):
+        for i in range(count):
+            rows = pl.ds(pl.multiple_of(first + i * experts, experts), experts)
+            best = jnp.maximum(best, jnp.abs(ref[rows, :]))
+        return best
+
+    def prepare(r, best):
         load_w(r).wait()
         rows = pl.ds(pl.multiple_of(r * tile, tile), tile)
         for at in range(0, 2 * half, tile):
@@ -191,6 +196,25 @@
                 wt_ref[device % 2, to : to + count, rows] = turned[done : done + count]
                 done += count
         wt_copy(r).start()
+        return largest(w_ref, r * tile, tile // experts, best)
+
+    choose = (
+        lax.broadcasted_iota(jnp.int32, (experts, experts), 0)
+        == jnp.broadcast_to(slot_ref[...], (experts, experts))
+    ).astype(F32).astype(BF16)
+    best = lax.fori_loop(0, blocks, prepare, jnp.zeros((experts, 2 * half), BF16))
+    s_pair[0, :, pl.ds(0, 2 * half)] = jnp.dot(
+        choose, best, preferred_element_type=F32
+    ).astype(BF16)
+    load_d.wait()
+    best = lax.fori_loop(
+        0, fl // 8, lambda r, held: largest(d_ref, r * 8 * experts, 8, held),
+        jnp.zeros((experts, width), BF16),
+    )
+    s_pair[0, :, pl.ds(2 * half, width)] = jnp.dot(
+        choose, best, preferred_element_type=F32
+    ).astype(BF16)
+    pair_copy.start()
 
     act_ref[...] = jnp.zeros_like(act_ref)
     spread_ref[...] = (
@@ -200,7 +224,6 @@
     for i in range(1, n):
         tok_copy(i).wait_recv()
     turned_ref[...] = tok_all[...].T
-    load_d.wait()
 
     def peer_of(bit):
         step = 1 << bit
@@ -248,7 +271,7 @@
         def _():
             run(usual)
 
-    def product(q):
+    def build(q):
         p, g = lax.rem(q, 2), q // 2
         lane = lax.broadcasted_iota(jnp.int32, (1, lanes), 1)
         spot = lax.rem(lane, span)
@@ -278,6 +301,7 @@
                     x_ref[side, at, :] = row.astype(BF16)
 
 
+    def product(q):
         h_ref[q] = jnp.dot(
             wt_ref[core], x_ref[core], preferred_element_type=F32
         ) + jnp.dot(wt_in[...], x_ref[1 - core], preferred_element_type=F32)
@@ -339,29 +363,6 @@
                 total_ += or_[g, across(i)].astype(F32)
             out32[g] = total_
 
-    def scales_in():
-        def up_max(r, best):
-            rows = pl.ds(pl.multiple_of(r * experts, experts), experts)
-            return jnp.maximum(best, jnp.abs(w_ref[rows, :]))
-
-        def down_max(r, best):
-            rows = pl.ds(pl.multiple_of(r * experts, experts), experts)
-            return jnp.maximum(best, jnp.abs(d_ref[rows, :]))
-
-        choose = (
-            lax.broadcasted_iota(jnp.int32, (experts, experts), 0)
-            == jnp.broadcast_to(slot_ref[...], (experts, experts))
-        ).astype(F32).astype(BF16)
-        best = lax.fori_loop(0, depth, up_max, jnp.zeros((experts, 2 * half), BF16))
-        s_pair[0, :, pl.ds(0, 2 * half)] = jnp.dot(
-            choose, best, preferred_element_type=F32
-        ).astype(BF16)
-        best = lax.fori_loop(0, fl, down_max, jnp.zeros((experts, width), BF16))
-        s_pair[0, :, pl.ds(2 * half, width)] = jnp.dot(
-            choose, best, preferred_element_type=F32
-        ).astype(BF16)
-        pair_copy.start()
-
     def scales_out():
         pair_copy.wait_recv()
         best = jnp.maximum(s_pair[0].astype(F32), s_pair[1].astype(F32))
@@ -370,17 +371,23 @@
         for i in range(1, m):
             scale_copy(i).start()
 
+    build(0)
+    scales_out()
     for r in range(blocks):
         wt_copy(r).wait_recv()
-    lags = [0] + [s + 1 for s in range(1, bits + 1)]
+    lags = [0] + [2 * s for s in range(1, bits + 1)]
     late = lags[bits]
 
-    @pl.loop(0, pieces + late + 2)
+    @pl.loop(0, pieces + late + 1)
     def _(step):
         @pl.when(step < pieces)
         def _():
             product(step)
             either(step, functools.partial(h_send, step, 0))
+
+        @pl.when(step < pieces - 1)
+        def _():
+            build(step + 1)
 
         for s in range(1, bits):
             @pl.when((step >= lags[s]) & (step < pieces + lags[s]))
@@ -396,17 +403,9 @@
         def _():
             o_send(step - late - 1)
 
-        @pl.when(step >= late + 2)
-        def _():
-            o_final(step - late - 2)
-
-        @pl.when(step == pieces)
-        def _():
-            scales_in()
-
-        @pl.when(step == pieces + 1)
-        def _():
-            scales_out()
+    @pl.loop(0, pieces)
+    def _(q):
+        o_final(q)
 
     out_ref[...] = jnp.concatenate([out32[g] for g in range(groups)], axis=0).astype(BF16)
     for i in range(1, m):

time: 80.8 us -> 73.8 us (0.913)
  Pallas kernels: 76.9 us -> 69.8 us
    pallas_call x1, Pallas kernels: 76.9 us -> 69.8 us  [fused(): pl.pallas_call(functools.partial(fused_kernel, (m, bits)), out_shape=(jax...]
where the time goes in v2:
time: 73.8 us; the launch traced here: 73.2 us
  Pallas kernels  69.8 us (95%)
  local copies, waits for them, and re-layouts  2.79 us (4%)
    pallas_call x1, Pallas kernels, fused(): pl.pallas_call(functools.partial(fused_kernel, (m, bits)), out_shape=(jax...  69.8 us
    unnamed x2, local copies, waits for them, and re-layouts  2.79 us

profile of v2, /device:TPU:0, one launch (start us, length us, event | category | flops | bytes accessed | tf_op | source)
XLA Modules:
  0.0 73.2 jit_solution(421285154365477154)
XLA Ops:
  0.6 69.8 %shard_map.77 = (bf16[16,2048]{1,0:T(8,128)(2,1)}, f32[1,3584]{1,0:T(1,128)}) custom-call(bf16[16,2048]{1,0:T(8,128)(2,1)} %tok_ref.1, s32[8,16]{1,0:T(8,128)} %bitcast.7, f32[8,16]{1,0:T(8,128)} %bitcast.8, s32[1,16]{1,0:T(1,128)} %bitcast.9, bf16[2048,1536]{1,0:T(8,128)(2,1)} %bitcast.5, bf16[768,2048]{1,0:T(8,128)(2,1)} %bitcast.6), custom_call_target="tpu_custom_call" | custom-call | tf_op jit(solution)/shard_map/pallas_call | solution.py:455
  70.4 1.5 %copy.10 = bf16[16,2048]{1,0:T(8,128)(2,1)} copy(bf16[16,2048]{1,0:T(8,128)(2,1)} %get-tuple-element.4) | data formatting | bytes 131072
  71.9 1.3 %copy.11 = f32[1,3584]{1,0:T(1,128)} copy(f32[1,3584]{1,0:T(1,128)} %get-tuple-element.5) | data formatting | bytes 28672

commit v3 on v2

--- a/solution.py
+++ b/solution.py
@@ -502,6 +502,21 @@
     )
 
 
+def settle_kernel(out_ref, scale_ref, out_to, scale_to):
+    out_to[...] = out_ref[...]
+    scale_to[...] = scale_ref[...]
+
+
+def settle(results):
+    vmem = pl.BlockSpec(memory_space=pltpu.VMEM)
+    return pl.pallas_call(
+        settle_kernel,
+        out_shape=tuple(jax.ShapeDtypeStruct(r.shape, r.dtype) for r in results),
+        in_specs=[vmem, vmem],
+        out_specs=(vmem, vmem),
+    )(*results)
+
+
 def layer(tokens, gate_up, down_proj, expert_ids, gate_weights, owner_slot):
     n = lax.axis_size("ep")
     own = tokens.shape[0]
@@ -513,7 +528,7 @@
         and n >= 4 and n * own * expert_ids.shape[1] % (256 * GROUPS) == 0
     )
     args = (tokens, gate_up, down_proj, expert_ids, gate_weights, owner_slot)
-    return fused(*args) if aligned and partials <= gate_up.size else shards(*args)
+    return settle(fused(*args)) if aligned and partials <= gate_up.size else shards(*args)
 
 
 def solution(mesh):

time: 73.8 us -> 72.5 us (0.982)
  local copies, waits for them, and re-layouts: 2.79 us -> 0 us
  Pallas kernels: 69.8 us -> 71.3 us
    unnamed x2 -> x0, local copies, waits for them, and re-layouts: 2.79 us -> none
    pallas_call x0 -> x1, Pallas kernels: none -> 1.48 us  [settle(): pl.pallas_call(settle_kernel, out_shape=tuple((jax.ShapeDtypeStruct(r.sha...]
where the time goes in v3:
time: 72.5 us; the launch traced here: 71.9 us
  Pallas kernels  71.3 us (98%)
    pallas_call x1, Pallas kernels, fused(): pl.pallas_call(functools.partial(fused_kernel, (m, bits)), out_shape=(jax...  69.8 us
    pallas_call x1, Pallas kernels, settle(): pl.pallas_call(settle_kernel, out_shape=tuple((jax.ShapeDtypeStruct(r.sha...  1.48 us

profile of v3, /device:TPU:0, one launch (start us, length us, event | category | flops | bytes accessed | tf_op | source)
XLA Modules:
  0.0 71.9 jit_solution(14653553500611679606)
XLA Ops:
  0.6 69.8 %shard_map.77 = (bf16[16,2048]{1,0:T(8,128)(2,1)}, f32[1,3584]{1,0:T(1,128)}) custom-call(bf16[16,2048]{1,0:T(8,128)(2,1)} %tok_ref.1, s32[8,16]{1,0:T(8,128)} %bitcast.7, f32[8,16]{1,0:T(8,128)} %bitcast.8, s32[1,16]{1,0:T(1,128)} %bitcast.9, bf16[2048,1536]{1,0:T(8,128)(2,1)} %bitcast.5, bf16[768,2048]{1,0:T(8,128)(2,1)} %bitcast.6), custom_call_target="tpu_custom_call" | custom-call | tf_op jit(solution)/shard_map/pallas_call | solution.py:455
  70.4 1.5 %shard_map.78 = (bf16[16,2048]{1,0:T(8,128)(2,1)}, f32[1,3584]{1,0:T(1,128)}) custom-call(bf16[16,2048]{1,0:T(8,128)(2,1)} %get-tuple-element.4.out_ref, f32[1,3584]{1,0:T(1,128)} %get-tuple-element.5.scale_ref), custom_call_target="tpu_custom_call" | custom-call | tf_op jit(solution)/shard_map/pallas_call | solution.py:512
